TPU v7x, 32 devices: a whole 2x2x4 slice. The times are simulated.
32 devices in a mesh: groups: 2 (over y), expert: 8 (over z, x), sub: 2 (over core).
Axes of the slice: x: 2, y: 2, z: 4, core: 2. Of those that a mesh axis runs over, the one named last changes fastest.
Arguments:
- stream_in: bfloat16 [1024, 3072], P(('groups', 'expert'), 'sub'), parts along dimension 0, may hold values from -0.29882812 to 0.29882812
- queries: bfloat16 [1024, 3072], P(('groups', 'expert'), 'sub'), parts along dimension 0, may hold values from -6 to 6
- kv_new: bfloat16 [2, 1024, 1024], P(None, ('groups', 'expert'), 'sub'), parts along dimension 1, may hold values from -6 to 6
- paged_key_value_cache: bfloat16 [2, 32, 4, 1024], P(None, ('groups', 'expert'), None, 'sub'), parts along dimension 1, may hold values from -6 to 6
- page_table: int32 [16, 8], P(('groups', 'expert')), parts along dimension 0, may hold values from 0 to 15, as said below
- prefix_len: int32 [16], P(('groups', 'expert')), parts along dimension 0, may hold values from 8 to 32
- norm_gain: float32 [3072], replicated, may hold values from 0.5 to 1.5
- w_router: bfloat16 [3072, 8], replicated, may hold values from -0.21875 to 0.21875
- expert_ids: int32 [1024, 2], P(('groups', 'expert')), parts along dimension 0, may hold values from 0 to 7, as said below
- w_in: bfloat16 [2, 3072, 65536], P(None, None, ('expert', 'sub')), may hold values from -0.109375 to 0.109375
Outputs:
- stream: bfloat16 [1024, 3072], P(('groups', 'expert'), 'sub'), parts along dimension 0
- expert_hidden: bfloat16 [272, 65536], P('groups', ('expert', 'sub')), parts along dimension 0
There are 2 independent parts, one for each index of `groups`. A program takes and returns all parts, laid end to end along the dimension named above; an argument that names none is the same for every part. Nothing has to cross between parts.
Inputs may be any that keep to these rules, and one draw needn't show every extreme that they name: `expert_ids`: each row names two different experts. The rows of one request name each expert at most 17 times, and one expert is named exactly 17 times by the rows of every request. `page_table`: the pages of one row lie in different shards: page // 2 differs along a row. Requests share leading pages.
All inputs are finite; a program needn't handle non-finite values.
Results may differ from a plain program's by a relative error of at most 0.018.
Values may be sent and summed in bfloat16 or wider, within the bound.
A program may use at most 128 MiB of HBM per device.

v0:
```python
import math
import jax
import jax.numpy as jnp
from jax import lax
from jax.sharding import PartitionSpec as P

HEAD_WIDTH = 128
EXPERTS = 8
TOP = 2
CAP = 17


def for_sending(array):

    def short(part):
        return part.astype(jnp.bfloat16) if part.dtype == jnp.float32 else part

    return jax.tree.map(short, array)


def partner(array, axis, apart):
    return lax.ppermute(array, axis, [(i, i ^ 1 << apart) for i in range(lax.axis_size(axis))])


def from_behind(value, axis, steps):
    count = lax.axis_size(axis)
    pairs = [(source, (source + steps) % count) for source in range(count)]
    return lax.ppermute(value, axis, pairs)


def attend(query_rows, key_rows, prefix_length, head_size):
    tokens_here = query_rows.shape[0]
    length = key_rows.shape[1]
    kv_heads = key_rows.shape[2] // head_size
    grouped = query_rows.shape[1] // head_size // kv_heads
    query_f = query_rows.reshape(tokens_here, kv_heads, grouped, head_size).astype(jnp.float32)
    keys_f = key_rows[0].reshape(length, kv_heads, head_size).astype(jnp.float32)
    values_f = key_rows[1].reshape(length, kv_heads, head_size).astype(jnp.float32)
    scores = jnp.einsum("tkgd,lkd->kgtl", query_f, keys_f) * (1.0 / math.sqrt(head_size))
    prefix_span = length - tokens_here
    places = jnp.arange(length)[None, :]
    rows_at = jnp.arange(tokens_here)[:, None]
    is_live = jnp.where(
        places < prefix_span, places < prefix_length, places - prefix_span <= rows_at
    )
    scores = jnp.where(is_live, scores, -1e30)
    largest = jnp.max(scores, axis=-1, keepdims=True)
    exponent = jnp.exp(scores - largest)
    weights = (exponent / jnp.sum(exponent, axis=-1, keepdims=True)).astype(jnp.bfloat16)
    mixed_heads = jnp.einsum("kgtl,lkd->tkgd", weights.astype(jnp.float32), values_f)
    return mixed_heads.reshape(tokens_here, -1).astype(jnp.bfloat16)


def pick_block(stack_rows, position):
    return lax.dynamic_index_in_dim(stack_rows, position, 0, keepdims=False)


def spread(kept_rows, kept_shares, own_index, level_values):
    for depth_bit in range(level_values):
        partner_rows, partner_shares = (
            partner(for_sending(kept_rows), "expert", depth_bit).astype(kept_rows.dtype),
            partner(for_sending(kept_shares), "expert", depth_bit).astype(kept_shares.dtype),
        )
        high_bit = (own_index >> depth_bit) % 2 == 1
        lower_rows = jnp.where(high_bit, partner_rows, kept_rows)
        upper_rows = jnp.where(high_bit, kept_rows, partner_rows)
        lower_shares = jnp.where(high_bit, partner_shares, kept_shares)
        upper_shares = jnp.where(high_bit, kept_shares, partner_shares)
        kept_rows = jnp.concatenate([lower_rows, upper_rows], axis=0)
        kept_shares = jnp.concatenate([lower_shares, upper_shares], axis=0)
    return (kept_rows, kept_shares)


def shards(
    stream_in,
    queries,
    kv_new,
    paged_key_value_cache,
    page_table,
    prefix_len,
    norm_gain,
    w_router,
    expert_ids,
    w_in,
):
    expert_count = lax.axis_size("expert")
    group_width = expert_count // EXPERTS
    level_values = group_width.bit_length() - 1
    own_index = lax.axis_index("expert")
    own_group = own_index // group_width
    shard_pages = paged_key_value_cache.shape[1]
    page_list = page_table[0]
    owners = page_list // shard_pages
    inside = page_list % shard_pages
    owner_hot = owners[None, :] == jnp.arange(expert_count, dtype=jnp.int32)[:, None]
    wanted = jnp.sum(jnp.where(owner_hot, inside[None, :], 0), axis=1)
    asked_for = lax.all_to_all(wanted[:, None], "expert", split_axis=0, concat_axis=0, tiled=True)
    served = jnp.take(paged_key_value_cache, asked_for[:, 0], axis=1)
    arrived = lax.all_to_all(served, "expert", split_axis=1, concat_axis=1, tiled=True)
    prefix_pages = jnp.take(arrived, owners, axis=1)
    prefix_row_block = prefix_pages.reshape(2, -1, prefix_pages.shape[-1])
    key_rows = jnp.concatenate([prefix_row_block, kv_new], axis=1)
    attended = attend(queries, key_rows, prefix_len[0], HEAD_WIDTH)
    stream_part = (stream_in.astype(jnp.float32) + attended.astype(jnp.float32)).astype(
        jnp.bfloat16
    )
    stream = lax.all_gather(stream_part, "sub", axis=1, tiled=True)
    stream_f = stream.astype(jnp.float32)
    scale_rows = lax.rsqrt(jnp.mean(stream_f * stream_f, axis=-1, keepdims=True) + 1e-05)
    normed = (stream_f * scale_rows * norm_gain).astype(jnp.bfloat16)
    logits = jnp.dot(normed, w_router, preferred_element_type=jnp.float32)
    chosen = jnp.take_along_axis(logits, expert_ids, axis=1)
    gate_share = jax.nn.sigmoid(chosen - chosen[:, ::-1])
    row_count = stream_in.shape[0]
    routes = expert_ids.reshape(-1)
    route_count = routes.shape[0]
    expert_hot = (routes[:, None] == jnp.arange(EXPERTS, dtype=jnp.int32)[None, :]).astype(
        jnp.int32
    )
    route_rank = jnp.sum((jnp.cumsum(expert_hot, axis=0) - 1) * expert_hot, axis=1)
    slot_hot = (route_rank[:, None] == jnp.arange(CAP, dtype=jnp.int32)[None, :]).astype(
        jnp.float32
    )
    row_hot = ((jnp.arange(route_count) // TOP)[:, None] == jnp.arange(row_count)[None, :]).astype(
        jnp.float32
    )
    route_place = expert_hot.astype(jnp.float32)[:, :, None] * slot_hot[:, None, :]
    picker = jnp.einsum("rem,rt->emt", route_place, row_hot)
    shares = jnp.einsum("rem,r->em", route_place, gate_share.reshape(-1))
    outgoing = jnp.einsum(
        "emt,td->emd", picker.astype(jnp.bfloat16), normed, preferred_element_type=jnp.float32
    ).astype(jnp.bfloat16)
    arrived_rows = [pick_block(outgoing, own_group)]
    arrived_shares = [pick_block(shares, own_group)]
    for stride in range(1, EXPERTS):
        target = (own_group + stride) % EXPERTS
        rows_in, shares_in = (
            from_behind(pick_block(outgoing, target), "expert", stride * group_width),
            from_behind(
                pick_block(shares, target).astype(jnp.bfloat16), "expert", stride * group_width
            ).astype(jnp.float32),
        )
        arrived_rows.append(rows_in)
        arrived_shares.append(shares_in)
    home_order = (own_group - jnp.arange(EXPERTS, dtype=jnp.int32)) % EXPERTS
    rows_by_source = jnp.take(jnp.stack(arrived_rows), home_order, axis=0)
    shares_by_source = jnp.take(jnp.stack(arrived_shares), home_order, axis=0)
    kept_rows, kept_shares = spread(
        rows_by_source[None], shares_by_source[None], own_index, level_values
    )
    slot_rows = kept_rows.reshape(-1, kept_rows.shape[-1])
    slot_shares = kept_shares.reshape(-1)
    gate_part = jnp.dot(slot_rows, w_in[0], preferred_element_type=jnp.float32)
    up_part = jnp.dot(slot_rows, w_in[1], preferred_element_type=jnp.float32)
    hidden = (jax.nn.silu(gate_part) * up_part * slot_shares[:, None]).astype(jnp.bfloat16)
    return (stream_part, hidden)


def solution(mesh):
    placed = (
        P(("groups", "expert"), "sub"),
        P(("groups", "expert"), "sub"),
        P(None, ("groups", "expert"), "sub"),
        P(None, ("groups", "expert"), None, "sub"),
        P(("groups", "expert"), None),
        P(("groups", "expert")),
        P(),
        P(),
        P(("groups", "expert"), None),
        P(None, None, ("expert", "sub")),
    )
    return jax.shard_map(
        shards,
        mesh=mesh,
        in_specs=placed,
        out_specs=(P(("groups", "expert"), "sub"), P("groups", ("expert", "sub"))),
        check_vma=False,
    )
```

profile of v0, /device:TPU:25, one launch (start us, length us, event | category | flops | bytes accessed | tf_op | source)
XLA Modules:
  0.0 103.8 jit_solution(13297511967904677882)
XLA Ops:
  0.7 0.7 fusion.77
  1.5 0.7 copy.83
  2.2 5.5 %all-to-all-start = ((s32[8,1,1]{2,1,0:T(1,128)}), s32[8,1,1]{2,1,0:T(1,128)S(1)}, u32[]{:S(2)}, u32[]{:S(2)}) async-start(s32[8,1,1]{2,1,0:T(1,128)} %copy.83), calls=%async_computation | async-start | bytes 8192 | tf_op jit(solution)/shard_map/all_to_all | solution.py:97
  7.7 0.7 fusion.60
  8.4 0.7 bitcast_or_fusion
  9.0 0.8 copy.90
  10.7 0.2 reduce_window_sum.11
  10.9 0.2 select_reduce_fusion
  11.1 0.2 reduce
  11.4 0.7 compare_and_fusion.1
  12.1 1.3 %gather_fusion = bf16[8,2,4,512]{3,2,1,0:T(4,128)(2,1)S(1)} fusion(bf16[2,2,4,512]{3,2,1,0:T(4,128)(2,1)} %param.13, s32[1024]{0:T(1024)S(1)} %pad_clamp_fusion.2), kind=kCustom, calls=%fused_computation | custom fusion | bytes 131104 | tf_op jit(solution)/shard_map/jit(_take)/gather | solution.py:98
  13.4 0.7 select_bitcast_fusion
  14.1 5.4 %all-to-all-start.1 = ((bf16[2,8,4,512]{3,2,0,1:T(4,128)(2,1)}), bf16[2,8,4,512]{3,2,0,1:T(4,128)(2,1)S(1)}, u32[]{:S(2)}, u32[]{:S(2)}) async-start(bf16[2,8,4,512]{3,2,0,1:T(4,128)(2,1)} %select_bitcast_fusion), calls=%async_computation.1 | async-start | bytes 131072 | tf_op jit(solution)/shard_map/all_to_all | solution.py:99
  20.2 2.1 %all-to-all-done.1 = bf16[2,8,4,512]{3,2,0,1:T(4,128)(2,1)S(1)} async-done(((bf16[2,8,4,512]{3,2,0,1:T(4,128)(2,1)}), bf16[2,8,4,512]{3,2,0,1:T(4,128)(2,1)S(1)}, u32[]{:S(2)}, u32[]{:S(2)}) %all-to-all-start.1) | async-done | bytes 65568 | tf_op jit(solution)/shard_map/all_to_all | solution.py:99
  22.3 0.6 gather_fusion.1
  23.2 0.4 fusion.81
  23.7 0.2 fusion.19
  23.9 1.4 %fusion.21 = f32[64,4,3,128]{3,0,2,1:T(8,128)S(1)} fusion(f32[4,3,64]{2,1,0:T(4,128)S(1)} %fusion.81, bf16[96,4,128,1]{2,1,0,3:T(4,128)(2,1)S(1)} %bitcast.148, f32[4,3,64,96]{3,2,1,0:T(8,128)S(1)} %fusion.19), kind=kOutput, calls=%fused_computation.24 | convolution fusion | flops 19293024 | bytes 789504 | tf_op jit(solution)/shard_map/kgtl,lkd->tkgd/dot_general | solution.py:50
  25.4 0.3 copy.89
  25.7 0.2 reshape.362
  25.9 0.4 copy-done.3
  26.4 4.6 %all_gather.3 = bf16[64,3072]{1,0:T(8,128)(2,1)S(1)} all-gather(bf16[64,1536]{1,0:T(8,128)(2,1)S(1)} %add_convert_fusion), channel_id=1, replica_groups=mesh['groups'=2,'expert'=8,'sub'=2] {'sub'}, dimensions={1}, use_global_device_ids=true | all-gather | bytes 589824 | tf_op jit(solution)/shard_map/all_gather | solution.py:107
  31.0 0.2 fusion.22
  31.2 0.3 fusion.32
  31.4 1.0 gather_fusion.4
  33.0 0.2 fusion.28
  33.3 1.0 collective-permute-start.13
  34.3 1.5 %collective-permute-start.12 = (bf16[17]{0:T(256)(128)(2,1)S(1)}, bf16[17]{0:T(256)(128)(2,1)S(1)}, u32[]{:S(2)}, u32[]{:S(2)}) collective-permute-start(bf16[17]{0:T(256)(128)(2,1)S(1)} %get-tuple-element.13), channel_id=1, source_target_pairs={{0,12},{2,14},{4,0},{6,2},{8,4},{10,6},{12,8},{14,10},{1,13},{3,15... | collective-permute-start | bytes 110 | tf_op jit(solution)/shard_map/ppermute | solution.py:28
  35.8 2.0 %collective-permute-start.11 = (bf16[17]{0:T(256)(128)(2,1)S(1)}, bf16[17]{0:T(256)(128)(2,1)S(1)}, u32[]{:S(2)}, u32[]{:S(2)}) collective-permute-start(bf16[17]{0:T(256)(128)(2,1)S(1)} %get-tuple-element.14), channel_id=1, source_target_pairs={{0,10},{2,12},{4,14},{6,0},{8,2},{10,4},{12,6},{14,8},{1,11},{3,13... | collective-permute-start | bytes 110 | tf_op jit(solution)/shard_map/ppermute | solution.py:28
  37.8 0.2 collective-permute-start.10
  38.0 2.4 %collective-permute-start.9 = (bf16[17]{0:T(256)(128)(2,1)S(1)}, bf16[17]{0:T(256)(128)(2,1)S(1)}, u32[]{:S(2)}, u32[]{:S(2)}) collective-permute-start(bf16[17]{0:T(256)(128)(2,1)S(1)} %get-tuple-element.16), channel_id=1, source_target_pairs={{0,6},{2,8},{4,10},{6,12},{8,14},{10,0},{12,2},{14,4},{1,7},{3,9},... | collective-permute-start | bytes 110 | tf_op jit(solution)/shard_map/ppermute | solution.py:28
  40.4 0.6 convolution_convert_fusion
  41.1 0.8 collective-permute-start.8
  42.0 1.0 collective-permute-start.7
  43.0 1.4 %collective-permute-start.6 = (bf16[17,3072]{1,0:T(8,128)(2,1)S(1)}, bf16[17,3072]{1,0:T(8,128)(2,1)S(1)}, u32[]{:S(2)}, u32[]{:S(2)}) collective-permute-start(bf16[17,3072]{1,0:T(8,128)(2,1)S(1)} %get-tuple-element.2), channel_id=1, source_target_pairs={{0,14},{2,0},{4,2},{6,4},{8,6},{10,8},{12,10},{14,12},{1,15},{3,1}... | collective-permute-start | bytes 313352 | tf_op jit(solution)/shard_map/ppermute | solution.py:28
  44.3 0.7 collective-permute-start.5
  45.1 2.9 %collective-permute-start.3 = (bf16[17,3072]{1,0:T(8,128)(2,1)S(1)}, bf16[17,3072]{1,0:T(8,128)(2,1)S(1)}, u32[]{:S(2)}, u32[]{:S(2)}) collective-permute-start(bf16[17,3072]{1,0:T(8,128)(2,1)S(1)} %get-tuple-element.5), channel_id=1, source_target_pairs={{0,8},{2,10},{4,12},{6,14},{8,0},{10,2},{12,4},{14,6},{1,9},{3,11}... | collective-permute-start | bytes 313352 | tf_op jit(solution)/shard_map/ppermute | solution.py:28
  48.0 1.2 %collective-permute-start = (bf16[17,3072]{1,0:T(8,128)(2,1)S(1)}, bf16[17,3072]{1,0:T(8,128)(2,1)S(1)}, u32[]{:S(2)}, u32[]{:S(2)}) collective-permute-start(bf16[17,3072]{1,0:T(8,128)(2,1)S(1)} %get-tuple-element.8), channel_id=1, source_target_pairs={{0,2},{2,4},{4,6},{6,8},{8,10},{10,12},{12,14},{14,0},{1,3},{3,5},... | collective-permute-start | bytes 313352 | tf_op jit(solution)/shard_map/ppermute | solution.py:28
  49.2 0.6 gather_fusion.3
  49.9 8.6 %collective-permute-done = bf16[17,3072]{1,0:T(8,128)(2,1)S(1)} collective-permute-done((bf16[17,3072]{1,0:T(8,128)(2,1)S(1)}, bf16[17,3072]{1,0:T(8,128)(2,1)S(1)}, u32[]{:S(2)}, u32[]{:S(2)}) %collective-permute-start) | collective-permute-done | bytes 104480 | tf_op jit(solution)/shard_map/ppermute | solution.py:28
  58.5 1.0 collective-permute-start.1
  59.5 11.4 %collective-permute-done.1 = bf16[17,3072]{1,0:T(8,128)(2,1)S(1)} collective-permute-done((bf16[17,3072]{1,0:T(8,128)(2,1)S(1)}, bf16[17,3072]{1,0:T(8,128)(2,1)S(1)}, u32[]{:S(2)}, u32[]{:S(2)}) %collective-permute-start.1) | collective-permute-done | bytes 104480 | tf_op jit(solution)/shard_map/ppermute | solution.py:28
  70.9 10.3 %collective-permute-done.2 = bf16[17,3072]{1,0:T(8,128)(2,1)S(1)} collective-permute-done((bf16[17,3072]{1,0:T(8,128)(2,1)S(1)}, bf16[17,3072]{1,0:T(8,128)(2,1)S(1)}, u32[]{:S(2)}, u32[]{:S(2)}) %collective-permute-start.2) | collective-permute-done | bytes 104480 | tf_op jit(solution)/shard_map/ppermute | solution.py:28
  81.3 0.6 gather_fusion.2
  81.9 0.2 broadcast_select_fusion
  82.1 0.3 select_n.256
  82.4 10.1 %fusion.3 = f32[136,4096]{1,0:T(8,128)S(1)} fusion(bf16[136,3072]{1,0:T(8,128)(2,1)S(1)} %select_n.256, bf16[2,3072,4096]{2,1,0:T(8,128)(2,1)} %param.19), kind=kOutput, calls=%fused_computation.8 | convolution fusion | flops 3422552064 | bytes 28229632 | tf_op jit(solution)/shard_map/dot_general | solution.py:153
  92.5 11.3 %fusion.13 = bf16[136,4096]{1,0:T(8,128)(2,1)} fusion(bf16[136,3072]{1,0:T(8,128)(2,1)S(1)} %select_n.256, bf16[2,3072,4096]{2,1,0:T(8,128)(2,1)} %param.19, f32[136,4096]{1,0:T(8,128)S(1)} %fusion.3, f32[136]{0:T(256)S(1)} %select_n.260), kind=kOutput, calls=%fused_computation.14 | convolution fusion | flops 3426451456 | bytes 29344288 | tf_op jit(solution)/shard_map/dot_general | solution.py:154
  (83 shorter events, 2.4 us)
Async XLA Ops:
  0.6 30.5 %copy-start = (bf16[3072,8]{0,1:T(8,128)(2,1)S(1)}, bf16[3072,8]{0,1:T(8,128)(2,1)}, u32[]{:S(2)}) copy-start(bf16[3072,8]{0,1:T(8,128)(2,1)} %param.17) | copy-start | bytes 147460
  0.6 19.2 %copy-start.2 = (bf16[64,1536]{1,0:T(8,128)(2,1)S(1)}, bf16[64,1536]{1,0:T(8,128)(2,1)}, u32[]{:S(2)}) copy-start(bf16[64,1536]{1,0:T(8,128)(2,1)} %param.11) | copy-start | bytes 589828
  0.7 22.5 %copy-start.4 = (bf16[2,64,512]{2,1,0:T(8,128)(2,1)S(1)}, bf16[2,64,512]{2,1,0:T(8,128)(2,1)}, u32[]{:S(2)}) copy-start(bf16[2,64,512]{2,1,0:T(8,128)(2,1)} %param.12) | copy-start | bytes 393220
  2.2 8.9 %all-to-all-start = ((s32[8,1,1]{2,1,0:T(1,128)}), s32[8,1,1]{2,1,0:T(1,128)S(1)}, u32[]{:S(2)}, u32[]{:S(2)}) async-start(s32[8,1,1]{2,1,0:T(1,128)} %copy.83), calls=%async_computation | async-start | bytes 8192 | tf_op jit(solution)/shard_map/all_to_all | solution.py:97
  14.1 8.2 %all-to-all-start.1 = ((bf16[2,8,4,512]{3,2,0,1:T(4,128)(2,1)}), bf16[2,8,4,512]{3,2,0,1:T(4,128)(2,1)S(1)}, u32[]{:S(2)}, u32[]{:S(2)}) async-start(bf16[2,8,4,512]{3,2,0,1:T(4,128)(2,1)} %select_bitcast_fusion), calls=%async_computation.1 | async-start | bytes 131072 | tf_op jit(solution)/shard_map/all_to_all | solution.py:99
  25.4 0.9 copy-start.3
  25.6 5.5 %copy-start.5 = (f32[3072]{0:T(1024)S(1)}, f32[3072]{0:T(1024)}, u32[]{:S(2)}) copy-start(f32[3072]{0:T(1024)} %param.16) | copy-start | bytes 36868
  26.3 6.1 %copy-start.1 = (bf16[64,1536]{1,0:T(8,128)(2,1)}, bf16[64,1536]{1,0:T(8,128)(2,1)S(1)}, u32[]{:S(2)}) copy-start(bf16[64,1536]{1,0:T(8,128)(2,1)S(1)} %add_convert_fusion) | copy-start | bytes 589828
  31.4 1.3 %copy-start.6 = (s32[64,2]{0,1:T(2,128)S(1)}, s32[64,2]{0,1:T(2,128)}, u32[]{:S(2)}) copy-start(s32[64,2]{0,1:T(2,128)} %param.18) | copy-start | bytes 1540
  33.3 7.8 %collective-permute-start.13 = (bf16[17]{0:T(256)(128)(2,1)S(1)}, bf16[17]{0:T(256)(128)(2,1)S(1)}, u32[]{:S(2)}, u32[]{:S(2)}) collective-permute-start(bf16[17]{0:T(256)(128)(2,1)S(1)} %get-tuple-element.12), channel_id=1, source_target_pairs={{0,14},{2,0},{4,2},{6,4},{8,6},{10,8},{12,10},{14,12},{1,15},{3,1}... | collective-permute-start | bytes 110 | tf_op jit(solution)/shard_map/ppermute | solution.py:28
  34.3 7.7 %collective-permute-start.12 = (bf16[17]{0:T(256)(128)(2,1)S(1)}, bf16[17]{0:T(256)(128)(2,1)S(1)}, u32[]{:S(2)}, u32[]{:S(2)}) collective-permute-start(bf16[17]{0:T(256)(128)(2,1)S(1)} %get-tuple-element.13), channel_id=1, source_target_pairs={{0,12},{2,14},{4,0},{6,2},{8,4},{10,6},{12,8},{14,10},{1,13},{3,15... | collective-permute-start | bytes 110 | tf_op jit(solution)/shard_map/ppermute | solution.py:28
  35.8 7.2 %collective-permute-start.11 = (bf16[17]{0:T(256)(128)(2,1)S(1)}, bf16[17]{0:T(256)(128)(2,1)S(1)}, u32[]{:S(2)}, u32[]{:S(2)}) collective-permute-start(bf16[17]{0:T(256)(128)(2,1)S(1)} %get-tuple-element.14), channel_id=1, source_target_pairs={{0,10},{2,12},{4,14},{6,0},{8,2},{10,4},{12,6},{14,8},{1,11},{3,13... | collective-permute-start | bytes 110 | tf_op jit(solution)/shard_map/ppermute | solution.py:28
  37.8 6.6 %collective-permute-start.10 = (bf16[17]{0:T(256)(128)(2,1)S(1)}, bf16[17]{0:T(256)(128)(2,1)S(1)}, u32[]{:S(2)}, u32[]{:S(2)}) collective-permute-start(bf16[17]{0:T(256)(128)(2,1)S(1)} %get-tuple-element.15), channel_id=1, source_target_pairs={{0,8},{2,10},{4,12},{6,14},{8,0},{10,2},{12,4},{14,6},{1,9},{3,11}... | collective-permute-start | bytes 110 | tf_op jit(solution)/shard_map/ppermute | solution.py:28
  38.0 7.0 %collective-permute-start.9 = (bf16[17]{0:T(256)(128)(2,1)S(1)}, bf16[17]{0:T(256)(128)(2,1)S(1)}, u32[]{:S(2)}, u32[]{:S(2)}) collective-permute-start(bf16[17]{0:T(256)(128)(2,1)S(1)} %get-tuple-element.16), channel_id=1, source_target_pairs={{0,6},{2,8},{4,10},{6,12},{8,14},{10,0},{12,2},{14,4},{1,7},{3,9},... | collective-permute-start | bytes 110 | tf_op jit(solution)/shard_map/ppermute | solution.py:28
  41.1 3.9 %collective-permute-start.8 = (bf16[17]{0:T(256)(128)(2,1)S(1)}, bf16[17]{0:T(256)(128)(2,1)S(1)}, u32[]{:S(2)}, u32[]{:S(2)}) collective-permute-start(bf16[17]{0:T(256)(128)(2,1)S(1)} %get-tuple-element.17), channel_id=1, source_target_pairs={{0,4},{2,6},{4,8},{6,10},{8,12},{10,14},{12,0},{14,2},{1,5},{3,7},... | collective-permute-start | bytes 110 | tf_op jit(solution)/shard_map/ppermute | solution.py:28
  42.0 6.0 %collective-permute-start.7 = (bf16[17]{0:T(256)(128)(2,1)S(1)}, bf16[17]{0:T(256)(128)(2,1)S(1)}, u32[]{:S(2)}, u32[]{:S(2)}) collective-permute-start(bf16[17]{0:T(256)(128)(2,1)S(1)} %get-tuple-element.18), channel_id=1, source_target_pairs={{0,2},{2,4},{4,6},{6,8},{8,10},{10,12},{12,14},{14,0},{1,3},{3,5},... | collective-permute-start | bytes 110 | tf_op jit(solution)/shard_map/ppermute | solution.py:28
  43.0 38.3 %collective-permute-start.6 = (bf16[17,3072]{1,0:T(8,128)(2,1)S(1)}, bf16[17,3072]{1,0:T(8,128)(2,1)S(1)}, u32[]{:S(2)}, u32[]{:S(2)}) collective-permute-start(bf16[17,3072]{1,0:T(8,128)(2,1)S(1)} %get-tuple-element.2), channel_id=1, source_target_pairs={{0,14},{2,0},{4,2},{6,4},{8,6},{10,8},{12,10},{14,12},{1,15},{3,1}... | collective-permute-start | bytes 313352 | tf_op jit(solution)/shard_map/ppermute | solution.py:28
  44.3 36.9 %collective-permute-start.5 = (bf16[17,3072]{1,0:T(8,128)(2,1)S(1)}, bf16[17,3072]{1,0:T(8,128)(2,1)S(1)}, u32[]{:S(2)}, u32[]{:S(2)}) collective-permute-start(bf16[17,3072]{1,0:T(8,128)(2,1)S(1)} %get-tuple-element.3), channel_id=1, source_target_pairs={{0,12},{2,14},{4,0},{6,2},{8,4},{10,6},{12,8},{14,10},{1,13},{3,15... | collective-permute-start | bytes 313352 | tf_op jit(solution)/shard_map/ppermute | solution.py:28
  45.0 36.2 %collective-permute-start.4 = (bf16[17,3072]{1,0:T(8,128)(2,1)S(1)}, bf16[17,3072]{1,0:T(8,128)(2,1)S(1)}, u32[]{:S(2)}, u32[]{:S(2)}) collective-permute-start(bf16[17,3072]{1,0:T(8,128)(2,1)S(1)} %get-tuple-element.4), channel_id=1, source_target_pairs={{0,10},{2,12},{4,14},{6,0},{8,2},{10,4},{12,6},{14,8},{1,11},{3,13... | collective-permute-start | bytes 313352 | tf_op jit(solution)/shard_map/ppermute | solution.py:28
  45.1 36.1 %collective-permute-start.3 = (bf16[17,3072]{1,0:T(8,128)(2,1)S(1)}, bf16[17,3072]{1,0:T(8,128)(2,1)S(1)}, u32[]{:S(2)}, u32[]{:S(2)}) collective-permute-start(bf16[17,3072]{1,0:T(8,128)(2,1)S(1)} %get-tuple-element.5), channel_id=1, source_target_pairs={{0,8},{2,10},{4,12},{6,14},{8,0},{10,2},{12,4},{14,6},{1,9},{3,11}... | collective-permute-start | bytes 313352 | tf_op jit(solution)/shard_map/ppermute | solution.py:28
  48.0 10.5 %collective-permute-start = (bf16[17,3072]{1,0:T(8,128)(2,1)S(1)}, bf16[17,3072]{1,0:T(8,128)(2,1)S(1)}, u32[]{:S(2)}, u32[]{:S(2)}) collective-permute-start(bf16[17,3072]{1,0:T(8,128)(2,1)S(1)} %get-tuple-element.8), channel_id=1, source_target_pairs={{0,2},{2,4},{4,6},{6,8},{8,10},{10,12},{12,14},{14,0},{1,3},{3,5},... | collective-permute-start | bytes 313352 | tf_op jit(solution)/shard_map/ppermute | solution.py:28
  58.5 12.4 %collective-permute-start.1 = (bf16[17,3072]{1,0:T(8,128)(2,1)S(1)}, bf16[17,3072]{1,0:T(8,128)(2,1)S(1)}, u32[]{:S(2)}, u32[]{:S(2)}) collective-permute-start(bf16[17,3072]{1,0:T(8,128)(2,1)S(1)} %get-tuple-element.7), channel_id=1, source_target_pairs={{0,4},{2,6},{4,8},{6,10},{8,12},{10,14},{12,0},{14,2},{1,5},{3,7},... | collective-permute-start | bytes 313352 | tf_op jit(solution)/shard_map/ppermute | solution.py:28
  70.9 10.3 %collective-permute-start.2 = (bf16[17,3072]{1,0:T(8,128)(2,1)S(1)}, bf16[17,3072]{1,0:T(8,128)(2,1)S(1)}, u32[]{:S(2)}, u32[]{:S(2)}) collective-permute-start(bf16[17,3072]{1,0:T(8,128)(2,1)S(1)} %get-tuple-element.6), channel_id=1, source_target_pairs={{0,6},{2,8},{4,10},{6,12},{8,14},{10,0},{12,2},{14,4},{1,7},{3,9},... | collective-permute-start | bytes 313352 | tf_op jit(solution)/shard_map/ppermute | solution.py:28
where the time goes:
time: 104 us
  waiting for transfers between devices  32.4 us (31%)
  starting transfers between devices  26.9 us (26%)
  matrix products  24.5 us (24%)
  local copies, waits for them, and re-layouts  8.52 us (8%)
  other arithmetic  5 us (5%)
  blocking collectives  4.6 us (4%)
  between operations  1.78 us (2%)
    ppermute x14, waiting for transfers between devices, from_behind(): return lax.ppermute(value, axis, pairs)  30.3 us
    ppermute x14, starting transfers between devices, from_behind(): return lax.ppermute(value, axis, pairs)  16 us
    dot_general x1, matrix products, shards(): up_part = jnp.dot(slot_rows, w_in[1], preferred_element_type=jnp.float32)  11.3 us
    dot_general x1, matrix products, shards(): gate_part = jnp.dot(slot_rows, w_in[0], preferred_element_type=jnp.float32)  10.1 us
    all_to_all x1, starting transfers between devices, shards(): lax.all_to_all(wanted[:, None], 'expert', split_axis=0, concat_axis=0, ti...  5.47 us
    all_to_all x1, starting transfers between devices, shards(): lax.all_to_all(served, 'expert', split_axis=1, concat_axis=1, tiled=True)  5.44 us
    all_gather x1, blocking collectives, shards(): stream = lax.all_gather(stream_part, 'sub', axis=1, tiled=True)  4.6 us
    all_to_all x1, waiting for transfers between devices, shards(): lax.all_to_all(served, 'expert', split_axis=1, concat_axis=1, tiled=True)  2.11 us
  transfers between devices with their start and end apart: 16, of which 4 were waited for; matrix products, arithmetic and copies ran while one was open for 5% of the time, Pallas kernels for 0%

commit v1 on v0

--- a/solution.py
+++ b/solution.py
@@ -3,6 +3,7 @@
 import jax.numpy as jnp
 from jax import lax
 from jax.sharding import PartitionSpec as P
+from jax.lax import all_to_all, axis_size
 
 HEAD_WIDTH = 128
 EXPERTS = 8
@@ -96,7 +97,15 @@
     wanted = jnp.sum(jnp.where(owner_hot, inside[None, :], 0), axis=1)
     asked_for = lax.all_to_all(wanted[:, None], "expert", split_axis=0, concat_axis=0, tiled=True)
     served = jnp.take(paged_key_value_cache, asked_for[:, 0], axis=1)
-    arrived = lax.all_to_all(served, "expert", split_axis=1, concat_axis=1, tiled=True)
+    arrived = jnp.concatenate(
+        all_to_all(
+            jnp.stack(jnp.split(served, axis_size("expert"), axis=1), axis=0),
+            concat_axis=0,
+            axis_name="expert",
+            split_axis=0,
+        ),
+        axis=1,
+    )
     prefix_pages = jnp.take(arrived, owners, axis=1)
     prefix_row_block = prefix_pages.reshape(2, -1, prefix_pages.shape[-1])
     key_rows = jnp.concatenate([prefix_row_block, kv_new], axis=1)

time: 104 us -> 108 us (1.038)
  local copies, waits for them, and re-layouts: 8.52 us -> 13.3 us
    unnamed x22 -> x29, local copies, waits for them, and re-layouts: 1.3 us -> 5.52 us
where the time goes in v1:
time: 108 us
  waiting for transfers between devices  32.4 us (30%)
  starting transfers between devices  26.9 us (25%)
  matrix products  24.5 us (23%)
  local copies, waits for them, and re-layouts  13.3 us (12%)
  blocking collectives  4.6 us (4%)
  other arithmetic  4.36 us (4%)
  between operations  1.78 us (2%)
    ppermute x14, waiting for transfers between devices, from_behind(): return lax.ppermute(value, axis, pairs)  30.3 us
    ppermute x14, starting transfers between devices, from_behind(): return lax.ppermute(value, axis, pairs)  16 us
    dot_general x1, matrix products, shards(): up_part = jnp.dot(slot_rows, w_in[1], preferred_element_type=jnp.float32)  11.3 us
    dot_general x1, matrix products, shards(): gate_part = jnp.dot(slot_rows, w_in[0], preferred_element_type=jnp.float32)  10.1 us
    unnamed x29, local copies, waits for them, and re-layouts  5.52 us
    all_to_all x1, starting transfers between devices, shards(): lax.all_to_all(wanted[:, None], 'expert', split_axis=0, concat_axis=0, ti...  5.47 us
    all_to_all x1, starting transfers between devices, shards(): all_to_all(jnp.stack(jnp.split(served, axis_size('expert'), axis=1), axis...  5.44 us
    all_gather x1, blocking collectives, shards(): stream = lax.all_gather(stream_part, 'sub', axis=1, tiled=True)  4.6 us
  transfers between devices with their start and end apart: 16, of which 4 were waited for; matrix products, arithmetic and copies ran while one was open for 5% of the time, Pallas kernels for 0%

profile of v1, /device:TPU:25, one launch (start us, length us, event | category | flops | bytes accessed | tf_op | source)
XLA Modules:
  0.0 108.0 jit_solution(3128092927539208967)
XLA Ops:
  0.7 0.7 fusion.77
  1.5 0.7 copy.83
  2.2 5.5 %all-to-all-start = ((s32[8,1,1]{2,1,0:T(1,128)}), s32[8,1,1]{2,1,0:T(1,128)S(1)}, u32[]{:S(2)}, u32[]{:S(2)}) async-start(s32[8,1,1]{2,1,0:T(1,128)} %copy.83), calls=%async_computation | async-start | bytes 8192 | tf_op jit(solution)/shard_map/all_to_all | solution.py:98
  7.7 0.7 fusion.60
  8.3 0.7 bitcast_or_fusion
  9.0 0.8 copy.90
  11.1 0.2 reduce
  11.3 0.7 compare_and_fusion.1
  12.0 1.3 %gather_fusion = bf16[8,2,4,512]{3,2,1,0:T(4,128)(2,1)S(1)} fusion(bf16[2,2,4,512]{3,2,1,0:T(4,128)(2,1)} %param.13, s32[1024]{0:T(1024)S(1)} %pad_clamp_fusion.2), kind=kCustom, calls=%fused_computation | custom fusion | bytes 131104 | tf_op jit(solution)/shard_map/jit(_take)/gather | solution.py:99
  13.5 0.6 constant_dynamic-update-slice_fusion.7
  14.1 0.6 constant_dynamic-update-slice_fusion.6
  14.7 0.6 constant_dynamic-update-slice_fusion.5
  15.3 0.6 constant_dynamic-update-slice_fusion.4
  15.9 0.6 constant_dynamic-update-slice_fusion.3
  16.5 0.6 constant_dynamic-update-slice_fusion.2
  17.1 0.6 constant_dynamic-update-slice_fusion.1
  17.7 0.6 constant_dynamic-update-slice_fusion
  18.3 5.4 %all-to-all-start.1 = ((bf16[8,2,1,4,512]{4,3,1,2,0:T(4,128)(2,1)}), bf16[8,2,1,4,512]{4,3,1,2,0:T(4,128)(2,1)S(1)}, u32[]{:S(2)}, u32[]{:S(2)}) async-start(bf16[8,2,1,4,512]{4,3,1,2,0:T(4,128)(2,1)} %constant_dynamic-update-slice_fusion), calls=%async_computation.1 | async-start | bytes 131072 | tf_op jit(solution)/shard_map/all_to_all | solution.py:101
  24.4 2.1 %all-to-all-done.1 = bf16[8,2,1,4,512]{4,3,1,2,0:T(4,128)(2,1)S(1)} async-done(((bf16[8,2,1,4,512]{4,3,1,2,0:T(4,128)(2,1)}), bf16[8,2,1,4,512]{4,3,1,2,0:T(4,128)(2,1)S(1)}, u32[]{:S(2)}, u32[]{:S(2)}) %all-to-all-start.1) | async-done | bytes 65568 | tf_op jit(solution)/shard_map/all_to_all | solution.py:101
  26.5 0.6 gather_fusion.1
  27.4 0.4 fusion.81
  28.1 1.4 %fusion.21 = f32[64,4,3,128]{3,0,2,1:T(8,128)S(1)} fusion(f32[4,3,64]{2,1,0:T(4,128)S(1)} %fusion.81, bf16[96,4,128,1]{2,1,0,3:T(4,128)(2,1)S(1)} %bitcast.184, f32[4,3,64,96]{3,2,1,0:T(8,128)S(1)} %fusion.19), kind=kOutput, calls=%fused_computation.24 | convolution fusion | flops 19293024 | bytes 789504 | tf_op jit(solution)/shard_map/kgtl,lkd->tkgd/dot_general | solution.py:51
  29.6 0.3 copy.89
  29.8 0.2 reshape.370
  30.1 0.4 copy-done.3
  30.5 4.6 %all_gather.3 = bf16[64,3072]{1,0:T(8,128)(2,1)S(1)} all-gather(bf16[64,1536]{1,0:T(8,128)(2,1)S(1)} %add_convert_fusion), channel_id=1, replica_groups=mesh['groups'=2,'expert'=8,'sub'=2] {'sub'}, dimensions={1}, use_global_device_ids=true | all-gather | bytes 589824 | tf_op jit(solution)/shard_map/all_gather | solution.py:116
  35.3 0.3 fusion.32
  35.6 1.0 gather_fusion.4
  37.5 1.0 collective-permute-start.13
  38.4 1.5 %collective-permute-start.12 = (bf16[17]{0:T(256)(128)(2,1)S(1)}, bf16[17]{0:T(256)(128)(2,1)S(1)}, u32[]{:S(2)}, u32[]{:S(2)}) collective-permute-start(bf16[17]{0:T(256)(128)(2,1)S(1)} %get-tuple-element.13), channel_id=1, source_target_pairs={{0,12},{2,14},{4,0},{6,2},{8,4},{10,6},{12,8},{14,10},{1,13},{3,15... | collective-permute-start | bytes 110 | tf_op jit(solution)/shard_map/ppermute | solution.py:29
  40.0 2.0 %collective-permute-start.11 = (bf16[17]{0:T(256)(128)(2,1)S(1)}, bf16[17]{0:T(256)(128)(2,1)S(1)}, u32[]{:S(2)}, u32[]{:S(2)}) collective-permute-start(bf16[17]{0:T(256)(128)(2,1)S(1)} %get-tuple-element.14), channel_id=1, source_target_pairs={{0,10},{2,12},{4,14},{6,0},{8,2},{10,4},{12,6},{14,8},{1,11},{3,13... | collective-permute-start | bytes 110 | tf_op jit(solution)/shard_map/ppermute | solution.py:29
  42.2 2.4 %collective-permute-start.9 = (bf16[17]{0:T(256)(128)(2,1)S(1)}, bf16[17]{0:T(256)(128)(2,1)S(1)}, u32[]{:S(2)}, u32[]{:S(2)}) collective-permute-start(bf16[17]{0:T(256)(128)(2,1)S(1)} %get-tuple-element.16), channel_id=1, source_target_pairs={{0,6},{2,8},{4,10},{6,12},{8,14},{10,0},{12,2},{14,4},{1,7},{3,9},... | collective-permute-start | bytes 110 | tf_op jit(solution)/shard_map/ppermute | solution.py:29
  44.6 0.6 convolution_convert_fusion
  45.3 0.8 collective-permute-start.8
  46.1 1.0 collective-permute-start.7
  47.2 1.4 %collective-permute-start.6 = (bf16[17,3072]{1,0:T(8,128)(2,1)S(1)}, bf16[17,3072]{1,0:T(8,128)(2,1)S(1)}, u32[]{:S(2)}, u32[]{:S(2)}) collective-permute-start(bf16[17,3072]{1,0:T(8,128)(2,1)S(1)} %get-tuple-element.2), channel_id=1, source_target_pairs={{0,14},{2,0},{4,2},{6,4},{8,6},{10,8},{12,10},{14,12},{1,15},{3,1}... | collective-permute-start | bytes 313352 | tf_op jit(solution)/shard_map/ppermute | solution.py:29
  48.5 0.7 collective-permute-start.5
  49.2 2.9 %collective-permute-start.3 = (bf16[17,3072]{1,0:T(8,128)(2,1)S(1)}, bf16[17,3072]{1,0:T(8,128)(2,1)S(1)}, u32[]{:S(2)}, u32[]{:S(2)}) collective-permute-start(bf16[17,3072]{1,0:T(8,128)(2,1)S(1)} %get-tuple-element.5), channel_id=1, source_target_pairs={{0,8},{2,10},{4,12},{6,14},{8,0},{10,2},{12,4},{14,6},{1,9},{3,11}... | collective-permute-start | bytes 313352 | tf_op jit(solution)/shard_map/ppermute | solution.py:29
  52.2 1.2 %collective-permute-start = (bf16[17,3072]{1,0:T(8,128)(2,1)S(1)}, bf16[17,3072]{1,0:T(8,128)(2,1)S(1)}, u32[]{:S(2)}, u32[]{:S(2)}) collective-permute-start(bf16[17,3072]{1,0:T(8,128)(2,1)S(1)} %get-tuple-element.8), channel_id=1, source_target_pairs={{0,2},{2,4},{4,6},{6,8},{8,10},{10,12},{12,14},{14,0},{1,3},{3,5},... | collective-permute-start | bytes 313352 | tf_op jit(solution)/shard_map/ppermute | solution.py:29
  53.4 0.6 gather_fusion.3
  54.1 8.6 %collective-permute-done = bf16[17,3072]{1,0:T(8,128)(2,1)S(1)} collective-permute-done((bf16[17,3072]{1,0:T(8,128)(2,1)S(1)}, bf16[17,3072]{1,0:T(8,128)(2,1)S(1)}, u32[]{:S(2)}, u32[]{:S(2)}) %collective-permute-start) | collective-permute-done | bytes 104480 | tf_op jit(solution)/shard_map/ppermute | solution.py:29
  62.7 1.0 collective-permute-start.1
  63.7 11.4 %collective-permute-done.1 = bf16[17,3072]{1,0:T(8,128)(2,1)S(1)} collective-permute-done((bf16[17,3072]{1,0:T(8,128)(2,1)S(1)}, bf16[17,3072]{1,0:T(8,128)(2,1)S(1)}, u32[]{:S(2)}, u32[]{:S(2)}) %collective-permute-start.1) | collective-permute-done | bytes 104480 | tf_op jit(solution)/shard_map/ppermute | solution.py:29
  75.1 10.3 %collective-permute-done.2 = bf16[17,3072]{1,0:T(8,128)(2,1)S(1)} collective-permute-done((bf16[17,3072]{1,0:T(8,128)(2,1)S(1)}, bf16[17,3072]{1,0:T(8,128)(2,1)S(1)}, u32[]{:S(2)}, u32[]{:S(2)}) %collective-permute-start.2) | collective-permute-done | bytes 104480 | tf_op jit(solution)/shard_map/ppermute | solution.py:29
  85.5 0.6 gather_fusion.2
  86.3 0.3 select_n.256
  86.6 10.1 %fusion.3 = f32[136,4096]{1,0:T(8,128)S(1)} fusion(bf16[136,3072]{1,0:T(8,128)(2,1)S(1)} %select_n.256, bf16[2,3072,4096]{2,1,0:T(8,128)(2,1)} %param.19), kind=kOutput, calls=%fused_computation.8 | convolution fusion | flops 3422552064 | bytes 28229632 | tf_op jit(solution)/shard_map/dot_general | solution.py:162
  96.7 11.3 %fusion.13 = bf16[136,4096]{1,0:T(8,128)(2,1)} fusion(bf16[136,3072]{1,0:T(8,128)(2,1)S(1)} %select_n.256, bf16[2,3072,4096]{2,1,0:T(8,128)(2,1)} %param.19, f32[136,4096]{1,0:T(8,128)S(1)} %fusion.3, f32[136]{0:T(256)S(1)} %select_n.260), kind=kOutput, calls=%fused_computation.14 | convolution fusion | flops 3426451456 | bytes 29344288 | tf_op jit(solution)/shard_map/dot_general | solution.py:163
  (91 shorter events, 3.8 us)
Async XLA Ops:
  0.6 34.7 %copy-start = (bf16[3072,8]{0,1:T(8,128)(2,1)S(1)}, bf16[3072,8]{0,1:T(8,128)(2,1)}, u32[]{:S(2)}) copy-start(bf16[3072,8]{0,1:T(8,128)(2,1)} %param.17) | copy-start | bytes 147460
  0.6 23.4 %copy-start.2 = (bf16[64,1536]{1,0:T(8,128)(2,1)S(1)}, bf16[64,1536]{1,0:T(8,128)(2,1)}, u32[]{:S(2)}) copy-start(bf16[64,1536]{1,0:T(8,128)(2,1)} %param.11) | copy-start | bytes 589828
  1.5 25.9 %copy-start.4 = (bf16[2,64,512]{2,1,0:T(8,128)(2,1)S(1)}, bf16[2,64,512]{2,1,0:T(8,128)(2,1)}, u32[]{:S(2)}) copy-start(bf16[2,64,512]{2,1,0:T(8,128)(2,1)} %param.12) | copy-start | bytes 393220
  2.2 8.9 %all-to-all-start = ((s32[8,1,1]{2,1,0:T(1,128)}), s32[8,1,1]{2,1,0:T(1,128)S(1)}, u32[]{:S(2)}, u32[]{:S(2)}) async-start(s32[8,1,1]{2,1,0:T(1,128)} %copy.83), calls=%async_computation | async-start | bytes 8192 | tf_op jit(solution)/shard_map/all_to_all | solution.py:98
  18.3 8.2 %all-to-all-start.1 = ((bf16[8,2,1,4,512]{4,3,1,2,0:T(4,128)(2,1)}), bf16[8,2,1,4,512]{4,3,1,2,0:T(4,128)(2,1)S(1)}, u32[]{:S(2)}, u32[]{:S(2)}) async-start(bf16[8,2,1,4,512]{4,3,1,2,0:T(4,128)(2,1)} %constant_dynamic-update-slice_fusion), calls=%async_computation.1 | async-start | bytes 131072 | tf_op jit(solution)/shard_map/all_to_all | solution.py:101
  29.6 0.9 copy-start.3
  29.8 5.5 %copy-start.5 = (f32[3072]{0:T(1024)S(1)}, f32[3072]{0:T(1024)}, u32[]{:S(2)}) copy-start(f32[3072]{0:T(1024)} %param.16) | copy-start | bytes 36868
  30.5 6.1 %copy-start.1 = (bf16[64,1536]{1,0:T(8,128)(2,1)}, bf16[64,1536]{1,0:T(8,128)(2,1)S(1)}, u32[]{:S(2)}) copy-start(bf16[64,1536]{1,0:T(8,128)(2,1)S(1)} %add_convert_fusion) | copy-start | bytes 589828
  35.6 1.3 %copy-start.6 = (s32[64,2]{0,1:T(2,128)S(1)}, s32[64,2]{0,1:T(2,128)}, u32[]{:S(2)}) copy-start(s32[64,2]{0,1:T(2,128)} %param.18) | copy-start | bytes 1540
  37.5 7.8 %collective-permute-start.13 = (bf16[17]{0:T(256)(128)(2,1)S(1)}, bf16[17]{0:T(256)(128)(2,1)S(1)}, u32[]{:S(2)}, u32[]{:S(2)}) collective-permute-start(bf16[17]{0:T(256)(128)(2,1)S(1)} %get-tuple-element.12), channel_id=1, source_target_pairs={{0,14},{2,0},{4,2},{6,4},{8,6},{10,8},{12,10},{14,12},{1,15},{3,1}... | collective-permute-start | bytes 110 | tf_op jit(solution)/shard_map/ppermute | solution.py:29
  38.4 7.7 %collective-permute-start.12 = (bf16[17]{0:T(256)(128)(2,1)S(1)}, bf16[17]{0:T(256)(128)(2,1)S(1)}, u32[]{:S(2)}, u32[]{:S(2)}) collective-permute-start(bf16[17]{0:T(256)(128)(2,1)S(1)} %get-tuple-element.13), channel_id=1, source_target_pairs={{0,12},{2,14},{4,0},{6,2},{8,4},{10,6},{12,8},{14,10},{1,13},{3,15... | collective-permute-start | bytes 110 | tf_op jit(solution)/shard_map/ppermute | solution.py:29
  40.0 7.2 %collective-permute-start.11 = (bf16[17]{0:T(256)(128)(2,1)S(1)}, bf16[17]{0:T(256)(128)(2,1)S(1)}, u32[]{:S(2)}, u32[]{:S(2)}) collective-permute-start(bf16[17]{0:T(256)(128)(2,1)S(1)} %get-tuple-element.14), channel_id=1, source_target_pairs={{0,10},{2,12},{4,14},{6,0},{8,2},{10,4},{12,6},{14,8},{1,11},{3,13... | collective-permute-start | bytes 110 | tf_op jit(solution)/shard_map/ppermute | solution.py:29
  42.0 6.6 %collective-permute-start.10 = (bf16[17]{0:T(256)(128)(2,1)S(1)}, bf16[17]{0:T(256)(128)(2,1)S(1)}, u32[]{:S(2)}, u32[]{:S(2)}) collective-permute-start(bf16[17]{0:T(256)(128)(2,1)S(1)} %get-tuple-element.15), channel_id=1, source_target_pairs={{0,8},{2,10},{4,12},{6,14},{8,0},{10,2},{12,4},{14,6},{1,9},{3,11}... | collective-permute-start | bytes 110 | tf_op jit(solution)/shard_map/ppermute | solution.py:29
  42.2 7.0 %collective-permute-start.9 = (bf16[17]{0:T(256)(128)(2,1)S(1)}, bf16[17]{0:T(256)(128)(2,1)S(1)}, u32[]{:S(2)}, u32[]{:S(2)}) collective-permute-start(bf16[17]{0:T(256)(128)(2,1)S(1)} %get-tuple-element.16), channel_id=1, source_target_pairs={{0,6},{2,8},{4,10},{6,12},{8,14},{10,0},{12,2},{14,4},{1,7},{3,9},... | collective-permute-start | bytes 110 | tf_op jit(solution)/shard_map/ppermute | solution.py:29
  45.3 3.9 %collective-permute-start.8 = (bf16[17]{0:T(256)(128)(2,1)S(1)}, bf16[17]{0:T(256)(128)(2,1)S(1)}, u32[]{:S(2)}, u32[]{:S(2)}) collective-permute-start(bf16[17]{0:T(256)(128)(2,1)S(1)} %get-tuple-element.17), channel_id=1, source_target_pairs={{0,4},{2,6},{4,8},{6,10},{8,12},{10,14},{12,0},{14,2},{1,5},{3,7},... | collective-permute-start | bytes 110 | tf_op jit(solution)/shard_map/ppermute | solution.py:29
  46.1 6.0 %collective-permute-start.7 = (bf16[17]{0:T(256)(128)(2,1)S(1)}, bf16[17]{0:T(256)(128)(2,1)S(1)}, u32[]{:S(2)}, u32[]{:S(2)}) collective-permute-start(bf16[17]{0:T(256)(128)(2,1)S(1)} %get-tuple-element.18), channel_id=1, source_target_pairs={{0,2},{2,4},{4,6},{6,8},{8,10},{10,12},{12,14},{14,0},{1,3},{3,5},... | collective-permute-start | bytes 110 | tf_op jit(solution)/shard_map/ppermute | solution.py:29
  47.2 38.3 %collective-permute-start.6 = (bf16[17,3072]{1,0:T(8,128)(2,1)S(1)}, bf16[17,3072]{1,0:T(8,128)(2,1)S(1)}, u32[]{:S(2)}, u32[]{:S(2)}) collective-permute-start(bf16[17,3072]{1,0:T(8,128)(2,1)S(1)} %get-tuple-element.2), channel_id=1, source_target_pairs={{0,14},{2,0},{4,2},{6,4},{8,6},{10,8},{12,10},{14,12},{1,15},{3,1}... | collective-permute-start | bytes 313352 | tf_op jit(solution)/shard_map/ppermute | solution.py:29
  48.5 36.9 %collective-permute-start.5 = (bf16[17,3072]{1,0:T(8,128)(2,1)S(1)}, bf16[17,3072]{1,0:T(8,128)(2,1)S(1)}, u32[]{:S(2)}, u32[]{:S(2)}) collective-permute-start(bf16[17,3072]{1,0:T(8,128)(2,1)S(1)} %get-tuple-element.3), channel_id=1, source_target_pairs={{0,12},{2,14},{4,0},{6,2},{8,4},{10,6},{12,8},{14,10},{1,13},{3,15... | collective-permute-start | bytes 313352 | tf_op jit(solution)/shard_map/ppermute | solution.py:29
  49.2 36.2 %collective-permute-start.4 = (bf16[17,3072]{1,0:T(8,128)(2,1)S(1)}, bf16[17,3072]{1,0:T(8,128)(2,1)S(1)}, u32[]{:S(2)}, u32[]{:S(2)}) collective-permute-start(bf16[17,3072]{1,0:T(8,128)(2,1)S(1)} %get-tuple-element.4), channel_id=1, source_target_pairs={{0,10},{2,12},{4,14},{6,0},{8,2},{10,4},{12,6},{14,8},{1,11},{3,13... | collective-permute-start | bytes 313352 | tf_op jit(solution)/shard_map/ppermute | solution.py:29
  49.2 36.1 %collective-permute-start.3 = (bf16[17,3072]{1,0:T(8,128)(2,1)S(1)}, bf16[17,3072]{1,0:T(8,128)(2,1)S(1)}, u32[]{:S(2)}, u32[]{:S(2)}) collective-permute-start(bf16[17,3072]{1,0:T(8,128)(2,1)S(1)} %get-tuple-element.5), channel_id=1, source_target_pairs={{0,8},{2,10},{4,12},{6,14},{8,0},{10,2},{12,4},{14,6},{1,9},{3,11}... | collective-permute-start | bytes 313352 | tf_op jit(solution)/shard_map/ppermute | solution.py:29
  52.2 10.5 %collective-permute-start = (bf16[17,3072]{1,0:T(8,128)(2,1)S(1)}, bf16[17,3072]{1,0:T(8,128)(2,1)S(1)}, u32[]{:S(2)}, u32[]{:S(2)}) collective-permute-start(bf16[17,3072]{1,0:T(8,128)(2,1)S(1)} %get-tuple-element.8), channel_id=1, source_target_pairs={{0,2},{2,4},{4,6},{6,8},{8,10},{10,12},{12,14},{14,0},{1,3},{3,5},... | collective-permute-start | bytes 313352 | tf_op jit(solution)/shard_map/ppermute | solution.py:29
  62.7 12.4 %collective-permute-start.1 = (bf16[17,3072]{1,0:T(8,128)(2,1)S(1)}, bf16[17,3072]{1,0:T(8,128)(2,1)S(1)}, u32[]{:S(2)}, u32[]{:S(2)}) collective-permute-start(bf16[17,3072]{1,0:T(8,128)(2,1)S(1)} %get-tuple-element.7), channel_id=1, source_target_pairs={{0,4},{2,6},{4,8},{6,10},{8,12},{10,14},{12,0},{14,2},{1,5},{3,7},... | collective-permute-start | bytes 313352 | tf_op jit(solution)/shard_map/ppermute | solution.py:29
  75.1 10.3 %collective-permute-start.2 = (bf16[17,3072]{1,0:T(8,128)(2,1)S(1)}, bf16[17,3072]{1,0:T(8,128)(2,1)S(1)}, u32[]{:S(2)}, u32[]{:S(2)}) collective-permute-start(bf16[17,3072]{1,0:T(8,128)(2,1)S(1)} %get-tuple-element.6), channel_id=1, source_target_pairs={{0,6},{2,8},{4,10},{6,12},{8,14},{10,0},{12,2},{14,4},{1,7},{3,9},... | collective-permute-start | bytes 313352 | tf_op jit(solution)/shard_map/ppermute | solution.py:29
